TPU v7x, 32 devices: a whole 2x2x4 slice. The times are simulated.
32 devices in a mesh: parts: 2 (over y), tile: 8 (over z, x), cond: 2 (over core).
Axes of the slice: x: 2, y: 2, z: 4, core: 2. Of those that a mesh axis runs over, the one named last changes fastest.
Arguments:
- mask: bfloat16 [16, 256, 256], P(('parts', 'tile')), parts along dimension 0, may hold values from -1 to 1
- kernels: bfloat16 [8, 24, 64, 128], P('cond'), may hold values from -6 to 6
- socs_weight: float32 [8, 24], P('cond'), may hold values from 0.02 to 1
- dose: float32 [8], P('cond'), may hold values from 0.8 to 1.25
- threshold: float32 [8], P('cond'), may hold values from 0.5 to 0.85
Outputs:
- band_max: float32 [16, 256, 256], P(('parts', 'tile'), 'cond'), parts along dimension 0
- band_min: float32 [16, 256, 256], P(('parts', 'tile'), 'cond'), parts along dimension 0
There are 2 independent parts, one for each index of `parts`. A program takes and returns all parts, laid end to end along the dimension named above; an argument that names none is the same for every part. Nothing has to cross between parts.
All inputs are finite; a program needn't handle non-finite values.
Results may differ from a plain program's by a relative error of at most 0.0068.
Values may be sent and summed in bfloat16 or wider, within the bound.
A program may use at most 64 MiB of HBM per device.

v0:
```python
import jax
import jax.numpy as jnp
import ml_dtypes
import numpy as np
from jax import lax
from jax.experimental import pallas as pl
from jax.experimental.pallas import tpu as pltpu
from jax.sharding import PartitionSpec as P

MARGIN = 64
BLUR = 8
GROUP = 24

diffusion = 2.0
steepness = 8.0
bf16 = jnp.bfloat16
f32 = jnp.float32


def trig(turns, period):
    angle = 2.0 * np.pi * (turns % period) / period
    return np.cos(angle), np.sin(angle)


def split(table):
    high = table.astype(ml_dtypes.bfloat16)
    low = (table - high.astype(np.float64)).astype(ml_dtypes.bfloat16)
    return high, low


def make_tables(core, band):
    pad = core + 2 * MARGIN
    grid = 2 * band
    freq = np.arange(band) - band // 2
    cos_in, sin_in = trig(np.arange(pad)[:, None] * freq[None, :], pad)
    order = np.r_[MARGIN : MARGIN + core, 0:MARGIN, MARGIN + core : pad]
    row_table = np.concatenate([cos_in[order].T, -sin_in[order].T], axis=0)
    both = np.concatenate([cos_in, sin_in], axis=1)
    left, inner, right = both[:MARGIN], both[MARGIN : MARGIN + core], both[MARGIN + core :]
    blank = np.zeros((core - MARGIN, 2 * band))
    send_table = np.concatenate(
        [inner, np.concatenate([blank, left]), np.concatenate([right, blank])], axis=1
    )
    zero = np.zeros_like(left)
    side_table = np.block([[left, zero], [zero, left], [right, zero], [zero, right]])
    cos_grid, sin_grid = trig(np.arange(grid)[:, None] * freq[None, :], grid)
    half_table = np.block([[cos_grid.T, sin_grid.T], [-sin_grid.T, cos_grid.T]])
    field_table = np.block([[cos_grid, -sin_grid], [sin_grid, cos_grid]])
    pixel = np.arange(core + 2 * BLUR) + MARGIN - BLUR
    phase = pixel[:, None] / pad - np.arange(grid)[None, :] / grid
    waves = np.arange(1, band)
    interp = (1.0 + 2.0 * np.cos(2.0 * np.pi * phase[:, :, None] * waves).sum(-1)) / grid
    offset = np.arange(core + 2 * BLUR)[None, :] - np.arange(core)[:, None] - BLUR
    taps = np.exp(-(offset**2) / (2.0 * diffusion**2)) * (np.abs(offset) <= BLUR)
    reach = np.arange(-BLUR, BLUR + 1)
    taps = taps / np.exp(-(reach**2) / (2.0 * diffusion**2)).sum()
    rise = taps @ interp
    high, low = split(rise)
    rise_rows = np.concatenate([high, high, low], axis=1)
    rise_cols = np.concatenate([high.T, high.T, low.T], axis=0)
    tables = (row_table, send_table, side_table, half_table, field_table)
    return (*(t.astype(ml_dtypes.bfloat16) for t in tables), rise_rows, rise_cols)


def neighbours():
    count = lax.axis_size("tile")
    columns = min(8, count // 2)
    rows = count // columns
    me = lax.axis_index("tile")
    position = lax.rem(me + columns // 2, count)
    column = lax.rem(position, columns)
    row = lax.div(position, columns)
    found = []
    for down in (-1, 0, 1):
        for right in (-1, 0, 1):
            if down == 0 and right == 0:
                continue
            flag = (row + down >= 0) & (row + down < rows)
            flag = flag & (column + right >= 0) & (column + right < columns)
            there = lax.rem(me + down * columns + right + count, count)
            found.append((down, right, flag, there))
    return found


def slot(down, right):
    return (0 if down < 0 else 1, right % 3) if down else (0 if right < 0 else 1,)


def high_low(value):
    high = value.astype(bf16)
    return high, (value - high.astype(f32)).astype(bf16)


def dot(a, b):
    return jnp.dot(a, b, preferred_element_type=f32)


def body(
    mask_hbm,
    kern_hbm,
    weight,
    dose,
    threshold,
    row_hbm,
    send_hbm,
    side_hbm,
    half_hbm,
    field_hbm,
    rise_rows_hbm,
    rise_cols_hbm,
    high_out,
    tile,
    kern,
    row_table,
    send_table,
    side_table,
    half_table,
    field_table,
    rise_rows,
    rise_cols,
    rows_out,
    rows_in,
    side_out,
    side_in,
    level,
    arrived,
    load_sem,
    kern_sem,
    halo_send,
    halo_recv,
    swap_send,
    swap_recv,
    halves,
    turned_kern,
):
    core = mask_hbm.shape[1]
    conds, kerns, band, _ = kern_hbm.shape
    grid = 2 * band
    n_cond = lax.axis_size("cond")
    me = lax.axis_index("cond")
    around = neighbours()

    loads = [
        pltpu.make_async_copy(src, dst, load_sem.at[i])
        for i, (src, dst) in enumerate(
            (
                (mask_hbm.at[0], tile),
                (row_hbm, row_table),
                (send_hbm, send_table),
                (side_hbm, side_table),
                (half_hbm, half_table),
                (field_hbm, field_table),
                (rise_rows_hbm, rise_rows),
                (rise_cols_hbm, rise_cols),
            )
        )
    ]
    loads[0].start()
    loads[1].start()
    loads[2].start()

    barrier = pltpu.get_barrier_semaphore()
    for _, _, flag, there in around:

        @pl.when(flag)
        def _():
            pl.semaphore_signal(barrier, inc=1, device_id={"tile": there})

    for step in range(1, n_cond):
        pl.semaphore_signal(barrier, inc=1, device_id={"cond": lax.rem(me + step, n_cond)})
    for load in loads[3:6]:
        load.start()
    for c in range(conds):
        pltpu.make_async_copy(kern_hbm.at[c], kern.at[c], kern_sem.at[c]).start()
    for load in loads[6:]:
        load.start()
    for down, right, flag, _ in around:

        @pl.when(jnp.logical_not(flag))
        def _():
            buffer = rows_in if down else side_in
            at = slot(down, right)
            buffer[at] = jnp.zeros(buffer.shape[len(at) :], bf16)

    for load in loads[:3]:
        load.wait()
    middle = dot(row_table[:, :core], tile[...]).astype(bf16)
    for at, first in ((0, 0), (1, core - MARGIN)):
        block = dot(tile[first : first + MARGIN, :], send_table[...]).astype(bf16)
        for lanes in range(3):
            rows_out[at, lanes] = block[:, lanes * 2 * band : (lanes + 1) * 2 * band]
        strip = middle[:, first : first + MARGIN]
        side_out[at] = jnp.concatenate([strip[:band], strip[band:]], axis=1)
    peers = n_cond - 1
    for _, _, flag, _ in around:
        peers = peers + flag.astype(jnp.int32)
    pl.semaphore_wait(barrier, peers)

    def halo(i):
        down, right, flag, there = around[i]
        outgoing, incoming = (rows_out, rows_in) if down else (side_out, side_in)
        return pltpu.make_async_remote_copy(
            src_ref=outgoing.at[slot(down, right)],
            dst_ref=incoming.at[slot(-down, -right)],
            send_sem=halo_send.at[i],
            recv_sem=halo_recv.at[len(around) - 1 - i],
            device_id={"tile": there},
        )

    def arrival(i):
        down, right, flag, there = around[i]
        outgoing, incoming = (rows_out, rows_in) if down else (side_out, side_in)
        return pltpu.make_async_remote_copy(
            src_ref=outgoing.at[slot(down, right)],
            dst_ref=incoming.at[slot(down, right)],
            send_sem=halo_send.at[i],
            recv_sem=halo_recv.at[i],
            device_id={"tile": there},
        )

    for i in range(len(around)):

        @pl.when(around[i][2])
        def _():
            halo(i).start()

    for load in loads[3:6]:
        load.wait()
    inner = dot(middle, send_table[:, : 2 * band])
    for c in range(conds):
        pltpu.make_async_copy(kern_hbm.at[c], kern.at[c], kern_sem.at[c]).wait()
    flat = kern[...].reshape(conds * kerns * band, 2 * band)
    turned_kern[...] = pltpu.roll(flat.astype(f32), band, 1).astype(bf16)

    for i in range(len(around)):

        @pl.when(around[i][2])
        def _():
            arrival(i).wait_recv()

    outer = rows_in[...].astype(f32)
    outer = (outer[:, 0] + outer[:, 1] + outer[:, 2]).reshape(2 * MARGIN, 2 * band).astype(bf16)
    sides = dot(jnp.concatenate([side_in[0], side_in[1]], axis=1), side_table[...])
    sides = jnp.concatenate([sides[:, : 2 * band], sides[:, 2 * band :]], axis=0)
    quarters = inner + dot(row_table[:, core:], outer) + sides
    quarters = quarters * (1.0 / ((core + 2 * MARGIN) * band))
    turned = pltpu.roll(quarters, band, 1)
    lane = lax.broadcasted_iota(jnp.int32, (band, 2 * band), 1)
    first = lane < band
    top, bottom = quarters[:band], quarters[band:]
    top_turned, bottom_turned = turned[:band], turned[band:]
    spec_same = jnp.where(first, top + bottom_turned, top_turned + bottom)
    spec_cross = jnp.where(first, top_turned - bottom, bottom_turned - top)

    def swap(c, step):
        return pltpu.make_async_remote_copy(
            src_ref=level.at[c],
            dst_ref=arrived.at[step - 1, c],
            send_sem=swap_send.at[step - 1, c],
            recv_sem=swap_recv.at[step - 1, c],
            device_id={"cond": lax.rem(me + step, n_cond)},
        )

    one = kern[...].reshape(conds * kerns, band, 2 * band).astype(f32)
    crossed = turned_kern[...].reshape(conds * kerns, band, 2 * band).astype(f32)
    prod = spec_same[None] * one + spec_cross[None] * crossed
    prod = prod.astype(bf16).reshape(conds * kerns * band, 2 * band)
    halves[...] = dot(prod, half_table[...]).astype(bf16)

    @pl.loop(0, conds)
    def _(c):
        total = jnp.zeros((grid, grid), f32)
        weight_sum = weight[c, 0]
        for k in range(1, kerns):
            weight_sum = weight_sum + weight[c, k]
        for start in range(0, kerns, GROUP):
            size = min(GROUP, kerns - start)
            rows = pl.multiple_of((c * kerns + start) * band, band)
            half = halves[pl.ds(rows, size * band), :]
            for k in range(0, size, 2):
                pair = [half[j * band : (j + 1) * band] for j in range(k, min(k + 2, size))]
                stacked = jnp.concatenate(
                    [
                        jnp.concatenate([h[:, :grid] for h in pair], axis=1),
                        jnp.concatenate([h[:, grid:] for h in pair], axis=1),
                    ],
                    axis=0,
                )
                field = dot(field_table[...], stacked)
                real, imag = field[:grid], field[grid:]
                power = real * real + imag * imag
                for j in range(len(pair)):
                    total = total + weight[c, start + k + j] * power[:, j * grid : (j + 1) * grid]
        gain = jnp.full((8, grid), steepness * dose[c], f32) / jnp.full((8, grid), weight_sum, f32)
        level[c] = total * gain[0:1] - steepness * threshold[c]
        for step in range(1, n_cond):
            swap(c, step).start()

    for load in loads[6:]:
        load.wait()
    share = high_out.shape[1]
    row_part = rise_rows[pl.ds(pl.multiple_of(me * share, share), share), :]
    bounds = None

    def include(bounds, value):
        high, low = high_low(value)
        wide = dot(jnp.concatenate([high, low, high], axis=1), rise_cols[...])
        high, low = high_low(wide)
        blurred = dot(row_part, jnp.concatenate([high, low, high], axis=0))
        if bounds is None:
            return blurred, blurred
        return jnp.maximum(bounds[0], blurred), jnp.minimum(bounds[1], blurred)

    for c in range(conds):
        bounds = include(bounds, level[c])
    for step in range(1, n_cond):
        for c in range(conds):
            swap(c, step).wait_recv()
            bounds = include(bounds, arrived[step - 1, c])
    high_out[0] = bounds[0]
    high_out[1] = bounds[1]
    for step in range(1, n_cond):
        for c in range(conds):
            swap(c, step).wait_send()
    for i in range(len(around)):

        @pl.when(around[i][2])
        def _():
            halo(i).wait_send()


def on_device(mask, kernels, socs_weight, dose, threshold):
    core = mask.shape[1]
    conds, kerns, band, _ = kernels.shape
    n_cond = lax.axis_size("cond")
    tables = [jnp.asarray(t) for t in make_tables(core, band)]
    share = core // n_cond
    out = jax.ShapeDtypeStruct((1, share, core), f32)
    anywhere = pl.BlockSpec(memory_space=pl.ANY)
    scalars = pl.BlockSpec(memory_space=pltpu.SMEM)
    vmem = pl.BlockSpec(memory_space=pltpu.VMEM)
    grid = 2 * band
    both = pl.pallas_call(
        body,
        out_shape=jax.ShapeDtypeStruct((2, share, core), f32),
        in_specs=[anywhere, anywhere, scalars, scalars, scalars] + [anywhere] * len(tables),
        out_specs=vmem,
        scratch_shapes=[
            pltpu.VMEM((core, core), bf16),
            pltpu.VMEM(kernels.shape, bf16),
            *[pltpu.VMEM(t.shape, bf16) for t in tables],
            pltpu.VMEM((2, 3, MARGIN, 2 * band), bf16),
            pltpu.VMEM((2, 3, MARGIN, 2 * band), bf16),
            pltpu.VMEM((2, band, 2 * MARGIN), bf16),
            pltpu.VMEM((2, band, 2 * MARGIN), bf16),
            pltpu.VMEM((conds, grid, grid), f32),
            pltpu.VMEM((n_cond - 1, conds, grid, grid), f32),
            pltpu.SemaphoreType.DMA((1 + len(tables),)),
            pltpu.SemaphoreType.DMA((conds,)),
            pltpu.SemaphoreType.DMA((8,)),
            pltpu.SemaphoreType.DMA((8,)),
            pltpu.SemaphoreType.DMA((n_cond - 1, conds)),
            pltpu.SemaphoreType.DMA((n_cond - 1, conds)),
            pltpu.VMEM((conds * kerns * band, 2 * grid), bf16),
            pltpu.VMEM((conds * kerns * band, 2 * band), bf16),
        ],
        compiler_params=pltpu.CompilerParams(collective_id=0, has_side_effects=True),
    )(mask, kernels, socs_weight, dose, threshold, *tables)
    both = jax.nn.sigmoid(both)
    return both[0:1], both[1:2]


def solution(mesh):
    return jax.shard_map(
        on_device,
        mesh=mesh,
        in_specs=(
            P(("parts", "tile"), None, None),
            P("cond", None, None, None),
            P("cond", None),
            P("cond"),
            P("cond"),
        ),
        out_specs=(P(("parts", "tile"), "cond", None), P(("parts", "tile"), "cond", None)),
        check_vma=False,
    )
```

profile of v0, /device:TPU:0, one launch (start us, length us, event | category | flops | bytes accessed | tf_op | source)
XLA Modules:
  0.0 19.0 jit_solution(8742193109605143391)
XLA Ops:
  0.6 16.6 %shard_map.131 = f32[2,128,256]{2,1,0:T(8,128)} custom-call(bf16[1,256,256]{2,1,0:T(8,128)(2,1)} %mask_hbm.1, bf16[4,24,64,128]{3,2,1,0:T(8,128)(2,1)} %kern_hbm.1, f32[4,24]{1,0:T(4,128)} %weight.1, f32[4]{0:T(128)} %dose.1, f32[4]{0:T(128)} %threshold.1, bf16[128,384]{1,0:T(8,128)(2,1)} %constant.16.clone.row_hbm, ...), custom_call_target="tpu_custom_call" | custom-call | tf_op jit(solution)/shard_map/pallas_call | solution.py:343
  17.3 1.0 %add_divide_fusion = f32[2,128,256]{2,1,0:T(8,128)S(1)} fusion(f32[2,128,256]{2,1,0:T(8,128)} %shard_map.131), kind=kLoop, calls=%fused_computation | loop fusion | flops 196608 | bytes 524288 | tf_op jit(solution)/shard_map/div | solution.py:369
  18.3 0.7 %fusion = (f32[1,128,256]{2,1,0:T(8,128)}, f32[1,128,256]{2,1,0:T(8,128)}) fusion(f32[2,128,256]{2,1,0:T(8,128)S(1)} %add_divide_fusion), kind=kLoop, calls=%fused_computation.1 | loop fusion | bytes 524288 | tf_op jit(solution)/shard_map/slice | solution.py:370
where the time goes:
time: 19.2 us; the launch traced here: 19 us
  Pallas kernels  16.6 us (86%)
  other arithmetic  1.03 us (5%)
  local copies, waits for them, and re-layouts  0.72 us (4%)
  between operations  0.64 us (3%)
    pallas_call x1, Pallas kernels, on_device(): pl.pallas_call(body, out_shape=jax.ShapeDtypeStruct((2, share, core), f32...  16.6 us
    div x1, other arithmetic, on_device(): both = jax.nn.sigmoid(both)  1.03 us
    slice x1, local copies, waits for them, and re-layouts, on_device(): return (both[0:1], both[1:2])  0.72 us

commit v1 on v0

--- a/solution.py
+++ b/solution.py
@@ -9,7 +9,8 @@
 
 MARGIN = 64
 BLUR = 8
-GROUP = 24
+GROUP = 4
+AHEAD = 2
 
 diffusion = 2.0
 steepness = 8.0
@@ -98,9 +99,9 @@
 def body(
     mask_hbm,
     kern_hbm,
-    weight,
-    dose,
-    threshold,
+    weight_hbm,
+    dose_hbm,
+    threshold_hbm,
     row_hbm,
     send_hbm,
     side_hbm,
@@ -109,6 +110,10 @@
     rise_rows_hbm,
     rise_cols_hbm,
     high_out,
+    low_out,
+    weight,
+    dose,
+    threshold,
     tile,
     kern,
     row_table,
@@ -125,13 +130,12 @@
     level,
     arrived,
     load_sem,
-    kern_sem,
     halo_send,
     halo_recv,
     swap_send,
     swap_recv,
-    halves,
-    turned_kern,
+    plain,
+    turned,
 ):
     core = mask_hbm.shape[1]
     conds, kerns, band, _ = kern_hbm.shape
@@ -147,6 +151,10 @@
                 (mask_hbm.at[0], tile),
                 (row_hbm, row_table),
                 (send_hbm, send_table),
+                (kern_hbm, kern),
+                (weight_hbm, weight),
+                (dose_hbm, dose),
+                (threshold_hbm, threshold),
                 (side_hbm, side_table),
                 (half_hbm, half_table),
                 (field_hbm, field_table),
@@ -155,9 +163,8 @@
             )
         )
     ]
-    loads[0].start()
-    loads[1].start()
-    loads[2].start()
+    for load in loads[:3]:
+        load.start()
 
     barrier = pltpu.get_barrier_semaphore()
     for _, _, flag, there in around:
@@ -168,11 +175,7 @@
 
     for step in range(1, n_cond):
         pl.semaphore_signal(barrier, inc=1, device_id={"cond": lax.rem(me + step, n_cond)})
-    for load in loads[3:6]:
-        load.start()
-    for c in range(conds):
-        pltpu.make_async_copy(kern_hbm.at[c], kern.at[c], kern_sem.at[c]).start()
-    for load in loads[6:]:
+    for load in loads[3:]:
         load.start()
     for down, right, flag, _ in around:
 
@@ -224,13 +227,21 @@
         def _():
             halo(i).start()
 
-    for load in loads[3:6]:
+    for load in loads[3:]:
         load.wait()
     inner = dot(middle, send_table[:, : 2 * band])
+    tops = []
     for c in range(conds):
-        pltpu.make_async_copy(kern_hbm.at[c], kern.at[c], kern_sem.at[c]).wait()
-    flat = kern[...].reshape(conds * kerns * band, 2 * band)
-    turned_kern[...] = pltpu.roll(flat.astype(f32), band, 1).astype(bf16)
+        weight_sum = weight[c, 0]
+        for k in range(1, kerns):
+            weight_sum = weight_sum + weight[c, k]
+        gain = jnp.full((8, grid), steepness * dose[c], f32) / jnp.full((8, grid), weight_sum, f32)
+        tops.append(steepness * threshold[c])
+        for k in range(kerns):
+            root = jnp.sqrt(gain * weight[c, k])
+            scaled = kern[c, k].astype(f32) * root[0:1]
+            plain[c, k] = scaled
+            turned[c, k] = pltpu.roll(scaled, band, 1)
 
     for i in range(len(around)):
 
@@ -244,11 +255,11 @@
     sides = jnp.concatenate([sides[:, : 2 * band], sides[:, 2 * band :]], axis=0)
     quarters = inner + dot(row_table[:, core:], outer) + sides
     quarters = quarters * (1.0 / ((core + 2 * MARGIN) * band))
-    turned = pltpu.roll(quarters, band, 1)
+    turned_quarters = pltpu.roll(quarters, band, 1)
     lane = lax.broadcasted_iota(jnp.int32, (band, 2 * band), 1)
     first = lane < band
     top, bottom = quarters[:band], quarters[band:]
-    top_turned, bottom_turned = turned[:band], turned[band:]
+    top_turned, bottom_turned = turned_quarters[:band], turned_quarters[band:]
     spec_same = jnp.where(first, top + bottom_turned, top_turned + bottom)
     spec_cross = jnp.where(first, top_turned - bottom, bottom_turned - top)
 
@@ -261,64 +272,73 @@
             device_id={"cond": lax.rem(me + step, n_cond)},
         )
 
-    one = kern[...].reshape(conds * kerns, band, 2 * band).astype(f32)
-    crossed = turned_kern[...].reshape(conds * kerns, band, 2 * band).astype(f32)
-    prod = spec_same[None] * one + spec_cross[None] * crossed
-    prod = prod.astype(bf16).reshape(conds * kerns * band, 2 * band)
-    halves[...] = dot(prod, half_table[...]).astype(bf16)
-
-    @pl.loop(0, conds)
-    def _(c):
-        total = jnp.zeros((grid, grid), f32)
-        weight_sum = weight[c, 0]
-        for k in range(1, kerns):
-            weight_sum = weight_sum + weight[c, k]
-        for start in range(0, kerns, GROUP):
-            size = min(GROUP, kerns - start)
-            rows = pl.multiple_of((c * kerns + start) * band, band)
-            half = halves[pl.ds(rows, size * band), :]
-            for k in range(0, size, 2):
-                pair = [half[j * band : (j + 1) * band] for j in range(k, min(k + 2, size))]
-                stacked = jnp.concatenate(
-                    [
-                        jnp.concatenate([h[:, :grid] for h in pair], axis=1),
-                        jnp.concatenate([h[:, grid:] for h in pair], axis=1),
-                    ],
-                    axis=0,
-                )
-                field = dot(field_table[...], stacked)
-                real, imag = field[:grid], field[grid:]
-                power = real * real + imag * imag
-                for j in range(len(pair)):
-                    total = total + weight[c, start + k + j] * power[:, j * grid : (j + 1) * grid]
-        gain = jnp.full((8, grid), steepness * dose[c], f32) / jnp.full((8, grid), weight_sum, f32)
-        level[c] = total * gain[0:1] - steepness * threshold[c]
-        for step in range(1, n_cond):
-            swap(c, step).start()
-
-    for load in loads[6:]:
-        load.wait()
+    def halves(c, start, size):
+        prod = [
+            (spec_same * plain[c, k] + spec_cross * turned[c, k]).astype(bf16)
+            for k in range(start, start + size)
+        ]
+        half = dot(jnp.concatenate(prod, axis=0), half_table[...]).astype(bf16)
+        return [half[j * band : (j + 1) * band] for j in range(size)]
+
+    def powers(total, pair):
+        stacked = jnp.concatenate(
+            [
+                jnp.concatenate([h[:, :grid] for h in pair], axis=1),
+                jnp.concatenate([h[:, grid:] for h in pair], axis=1),
+            ],
+            axis=0,
+        )
+        field = dot(field_table[...], stacked)
+        power = field[:grid] * field[:grid] + field[grid:] * field[grid:]
+        for j in range(len(pair)):
+            total = total + power[:, j * grid : (j + 1) * grid]
+        return total
+
+    groups = [
+        (c, start, min(GROUP, kerns - start)) for c in range(conds) for start in range(0, kerns, GROUP)
+    ]
+    ready = [halves(*groups[i]) for i in range(min(AHEAD, len(groups)))]
+    total = None
+    for i, (c, start, size) in enumerate(groups):
+        if i + AHEAD < len(groups):
+            ready.append(halves(*groups[i + AHEAD]))
+        if start == 0:
+            total = jnp.full((grid, grid), -tops[c], f32)
+        half = ready[i]
+        for j in range(0, size, 2):
+            total = powers(total, half[j : j + 2])
+        if start + size == kerns:
+            level[c] = total
+            for step in range(1, n_cond):
+                swap(c, step).start()
+
     share = high_out.shape[1]
     row_part = rise_rows[pl.ds(pl.multiple_of(me * share, share), share), :]
-    bounds = None
-
-    def include(bounds, value):
-        high, low = high_low(value)
+
+    def include(bounds, values):
+        high, low = high_low(jnp.concatenate(values, axis=0))
         wide = dot(jnp.concatenate([high, low, high], axis=1), rise_cols[...])
         high, low = high_low(wide)
+        high = jnp.concatenate([high[j * grid : (j + 1) * grid] for j in range(len(values))], axis=1)
+        low = jnp.concatenate([low[j * grid : (j + 1) * grid] for j in range(len(values))], axis=1)
         blurred = dot(row_part, jnp.concatenate([high, low, high], axis=0))
-        if bounds is None:
-            return blurred, blurred
-        return jnp.maximum(bounds[0], blurred), jnp.minimum(bounds[1], blurred)
-
-    for c in range(conds):
-        bounds = include(bounds, level[c])
-    for step in range(1, n_cond):
-        for c in range(conds):
-            swap(c, step).wait_recv()
-            bounds = include(bounds, arrived[step - 1, c])
+        for j in range(len(values)):
+            one = blurred[:, j * core : (j + 1) * core]
+            bounds = (one, one) if bounds is None else (
+                jnp.maximum(bounds[0], one),
+                jnp.minimum(bounds[1], one),
+            )
+        return bounds
+
+    bounds = include(None, [level[c] for c in range(conds)])
+    pieces = [(step, c) for step in range(1, n_cond) for c in range(conds)]
+    for some in (pieces[:-1], pieces[-1:]):
+        if some:
+            for step, c in some:
+                swap(c, step).wait_recv()
+            bounds = include(bounds, [arrived[step - 1, c] for step, c in some])
     high_out[0] = bounds[0]
-    high_out[1] = bounds[1]
+    low_out[0] = bounds[1]
     for step in range(1, n_cond):
         for c in range(conds):
             swap(c, step).wait_send()
@@ -335,17 +355,19 @@
     n_cond = lax.axis_size("cond")
     tables = [jnp.asarray(t) for t in make_tables(core, band)]
     share = core // n_cond
-    out = jax.ShapeDtypeStruct((1, share, core), f32)
     anywhere = pl.BlockSpec(memory_space=pl.ANY)
-    scalars = pl.BlockSpec(memory_space=pltpu.SMEM)
     vmem = pl.BlockSpec(memory_space=pltpu.VMEM)
     grid = 2 * band
-    both = pl.pallas_call(
+    out = pltpu.VMEM((1, share, core), f32)
+    high, low = pl.pallas_call(
         body,
-        out_shape=jax.ShapeDtypeStruct((2, share, core), f32),
-        in_specs=[anywhere, anywhere, scalars, scalars, scalars] + [anywhere] * len(tables),
-        out_specs=vmem,
+        out_shape=(out, out),
+        in_specs=[anywhere] * (5 + len(tables)),
+        out_specs=(vmem, vmem),
         scratch_shapes=[
+            pltpu.SMEM(socs_weight.shape, f32),
+            pltpu.SMEM(dose.shape, f32),
+            pltpu.SMEM(threshold.shape, f32),
             pltpu.VMEM((core, core), bf16),
             pltpu.VMEM(kernels.shape, bf16),
             *[pltpu.VMEM(t.shape, bf16) for t in tables],
@@ -355,19 +377,17 @@
             pltpu.VMEM((2, band, 2 * MARGIN), bf16),
             pltpu.VMEM((conds, grid, grid), f32),
             pltpu.VMEM((n_cond - 1, conds, grid, grid), f32),
-            pltpu.SemaphoreType.DMA((1 + len(tables),)),
-            pltpu.SemaphoreType.DMA((conds,)),
+            pltpu.SemaphoreType.DMA((5 + len(tables),)),
             pltpu.SemaphoreType.DMA((8,)),
             pltpu.SemaphoreType.DMA((8,)),
             pltpu.SemaphoreType.DMA((n_cond - 1, conds)),
             pltpu.SemaphoreType.DMA((n_cond - 1, conds)),
-            pltpu.VMEM((conds * kerns * band, 2 * grid), bf16),
-            pltpu.VMEM((conds * kerns * band, 2 * band), bf16),
+            pltpu.VMEM(kernels.shape, f32),
+            pltpu.VMEM(kernels.shape, f32),
         ],
         compiler_params=pltpu.CompilerParams(collective_id=0, has_side_effects=True),
     )(mask, kernels, socs_weight, dose, threshold, *tables)
-    both = jax.nn.sigmoid(both)
-    return both[0:1], both[1:2]
+    return jax.nn.sigmoid(high), jax.nn.sigmoid(low)
 
 
 def solution(mesh):

time: 19.2 us -> 16.2 us (0.84)
  Pallas kernels: 16.6 us -> 14.6 us
  local copies, waits for them, and re-layouts: 0.72 us -> 0 us
  other arithmetic: 1.03 us -> 0.77 us
    pallas_call x1, Pallas kernels: 16.6 us -> 14.6 us  [on_device(): pl.pallas_call(body, out_shape=(out, out), in_specs=[anywhere] * (5 + len...]
    slice x1 -> x0, local copies, waits for them, and re-layouts: 0.72 us -> none  [on_device(): return (both[0:1], both[1:2])]
    div x1, other arithmetic: 1.03 us -> 0.77 us  [on_device(): return (jax.nn.sigmoid(high), jax.nn.sigmoid(low))]
where the time goes in v1:
time: 16.2 us; the launch traced here: 16 us
  Pallas kernels  14.6 us (90%)
  other arithmetic  0.77 us (5%)
  between operations  0.64 us (4%)
    pallas_call x1, Pallas kernels, on_device(): pl.pallas_call(body, out_shape=(out, out), in_specs=[anywhere] * (5 + len...  14.6 us
    div x1, other arithmetic, on_device(): return (jax.nn.sigmoid(high), jax.nn.sigmoid(low))  0.77 us

profile of v1, /device:TPU:0, one launch (start us, length us, event | category | flops | bytes accessed | tf_op | source)
XLA Modules:
  0.0 16.0 jit_solution(1730397914935213865)
XLA Ops:
  0.6 14.6 %shard_map.131 = (f32[1,128,256]{2,1,0:T(8,128)S(1)}, f32[1,128,256]{2,1,0:T(8,128)S(1)}) custom-call(bf16[1,256,256]{2,1,0:T(8,128)(2,1)} %mask_hbm.1, bf16[4,24,64,128]{3,2,1,0:T(8,128)(2,1)} %kern_hbm.1, f32[4,24]{1,0:T(4,128)} %weight_hbm.1, f32[4]{0:T(128)} %dose_hbm.1, f32[4]{0:T(128)} %threshold_hbm.1, bf16[128,384]{1,0:T(8,128)(2,1)} %constant.16.clone.row_hbm, ...), custom_call_target="tpu_custom_call" | custom-call | tf_op jit(solution)/shard_map/pallas_call | solution.py:362
  15.2 0.8 %add_divide_fusion = (f32[1,128,256]{2,1,0:T(8,128)}, f32[1,128,256]{2,1,0:T(8,128)}) fusion(f32[1,128,256]{2,1,0:T(8,128)S(1)} %get-tuple-element.5, f32[1,128,256]{2,1,0:T(8,128)S(1)} %get-tuple-element.4), kind=kLoop, calls=%fused_computation | loop fusion | flops 196608 | bytes 524288 | tf_op jit(solution)/shard_map/div | solution.py:390

commit v2 on v1

v2 whole, which is shorter than its diff:
```python
import functools

import jax
import jax.numpy as jnp
import ml_dtypes
import numpy as np
from jax import lax
from jax.experimental import pallas as pl
from jax.experimental.pallas import tpu as pltpu
from jax.sharding import PartitionSpec as P

MARGIN = 64
BLUR = 8
GROUP = 4
AHEAD = 2
DELAY = 2

diffusion = 2.0
steepness = 8.0
bf16 = jnp.bfloat16
f32 = jnp.float32


def trig(turns, period):
    angle = 2.0 * np.pi * (turns % period) / period
    return np.cos(angle), np.sin(angle)


def split(table):
    high = table.astype(ml_dtypes.bfloat16)
    low = (table - high.astype(np.float64)).astype(ml_dtypes.bfloat16)
    return high, low


def make_tables(core, band):
    pad = core + 2 * MARGIN
    grid = 2 * band
    freq = np.arange(band) - band // 2
    cos_in, sin_in = trig(np.arange(pad)[:, None] * freq[None, :], pad)
    order = np.r_[MARGIN : MARGIN + core, 0:MARGIN, MARGIN + core : pad]
    row_table = np.concatenate([cos_in[order].T, -sin_in[order].T], axis=0)
    both = np.concatenate([cos_in, sin_in], axis=1)
    left, inner, right = both[:MARGIN], both[MARGIN : MARGIN + core], both[MARGIN + core :]
    zero = np.zeros_like(left)
    gap = np.zeros((core - 2 * MARGIN, 2 * band))
    edges = np.concatenate([right, gap, left], axis=0)
    first_table = np.concatenate(
        [row_table[:, :core], np.concatenate([inner, edges], axis=1)], axis=0
    )
    side_table = np.block([[left, zero], [zero, left], [right, zero], [zero, right]])
    cos_grid, sin_grid = trig(np.arange(grid)[:, None] * freq[None, :], grid)
    half_table = np.block([[cos_grid.T, sin_grid.T], [-sin_grid.T, cos_grid.T]])
    field_table = np.concatenate(
        [np.concatenate([cos_grid, -sin_grid], axis=1), np.concatenate([sin_grid, cos_grid], axis=1)], axis=1
    )
    pixel = np.arange(core + 2 * BLUR) + MARGIN - BLUR
    phase = pixel[:, None] / pad - np.arange(grid)[None, :] / grid
    waves = np.arange(1, band)
    interp = (1.0 + 2.0 * np.cos(2.0 * np.pi * phase[:, :, None] * waves).sum(-1)) / grid
    offset = np.arange(core + 2 * BLUR)[None, :] - np.arange(core)[:, None] - BLUR
    taps = np.exp(-(offset**2) / (2.0 * diffusion**2)) * (np.abs(offset) <= BLUR)
    reach = np.arange(-BLUR, BLUR + 1)
    taps = taps / np.exp(-(reach**2) / (2.0 * diffusion**2)).sum()
    rise = taps @ interp
    high, low = split(rise)
    rise_rows = np.concatenate([high, low], axis=1)
    rise_cols = np.concatenate([high.T, low.T], axis=0)
    outer_rows = np.concatenate([row_table[:, core:], np.zeros((2 * band, 2 * band))], axis=1)
    later = (side_table, half_table, field_table, outer_rows, rise_cols, rise_rows)
    bounds = np.cumsum([0] + [len(t) for t in later])
    later = np.concatenate([t.astype(ml_dtypes.bfloat16) for t in later], axis=0)
    return first_table.astype(ml_dtypes.bfloat16), later, [int(n) for n in bounds]


def neighbours():
    count = lax.axis_size("tile")
    columns = min(8, count // 2)
    rows = count // columns
    me = lax.axis_index("tile")
    position = lax.rem(me + columns // 2, count)
    column = lax.rem(position, columns)
    row = lax.div(position, columns)
    found = []
    for down in (-1, 0, 1):
        for right in (-1, 0, 1):
            if down == 0 and right == 0:
                continue
            flag = (row + down >= 0) & (row + down < rows)
            flag = flag & (column + right >= 0) & (column + right < columns)
            there = lax.rem(me + down * columns + right + count, count)
            found.append((down, right, flag, there))
    return found


def slot(down, right):
    return (0 if down < 0 else 1, right % 3) if down else (0 if right < 0 else 1,)


def high_low(value):
    high = value.astype(bf16)
    return high, (value - high.astype(f32)).astype(bf16)


def dot(a, b):
    return jnp.dot(a, b, preferred_element_type=f32)


def body(
    parts,
    mask_hbm,
    kern_hbm,
    weight_hbm,
    dose_hbm,
    threshold_hbm,
    first_hbm,
    later_hbm,
    high_out,
    low_out,
    weight,
    dose,
    threshold,
    tile,
    kern,
    first_table,
    later_table,
    rows_out,
    rows_in,
    side_out,
    side_in,
    level,
    arrived,
    load_sem,
    halo_send,
    halo_recv,
    swap_send,
    swap_recv,
    plain,
    turned,
):
    core = mask_hbm.shape[1]
    conds, kerns, band, _ = kern_hbm.shape
    grid = 2 * band
    middle_of = core // 2
    n_cond = lax.axis_size("cond")
    me = lax.axis_index("cond")
    near = n_cond - 1
    sender = me == near
    around = neighbours()
    side_table, half_table, field_table, outer_rows, rise_cols, rise_rows = (
        later_table.at[pl.ds(lo, hi - lo)] for lo, hi in zip(parts[:-1], parts[1:])
    )
    row_table = first_table.at[pl.ds(0, grid)]
    inner_table = first_table.at[pl.ds(grid, core), pl.ds(0, grid)]
    edge_table = first_table.at[pl.ds(grid, core), pl.ds(grid, grid)]

    loads = [
        pltpu.make_async_copy(src, dst, load_sem.at[i])
        for i, (src, dst) in enumerate(
            (
                (mask_hbm.at[0], tile),
                (first_hbm, first_table),
                (kern_hbm, kern),
                (weight_hbm, weight),
                (dose_hbm, dose),
                (threshold_hbm, threshold),
                (later_hbm, later_table),
            )
        )
    ]
    for load in loads[:2]:
        load.start()

    barrier = pltpu.get_barrier_semaphore()
    for _, _, flag, there in around:

        @pl.when(flag)
        def _():
            pl.semaphore_signal(barrier, inc=1, device_id={"tile": there, "cond": near})

    for step in range(1, n_cond):
        pl.semaphore_signal(barrier, inc=1, device_id={"cond": lax.rem(me + step, n_cond)})
    for down, right, flag, _ in around:

        @pl.when(jnp.logical_not(flag))
        def _():
            buffer = rows_in if down else side_in
            at = slot(down, right)
            buffer[at] = jnp.zeros(buffer.shape[len(at) :], bf16)

    for load in loads[:2]:
        load.wait()
    for load in loads[2:]:
        load.start()
    strips = jnp.concatenate([tile[:MARGIN, :], tile[core - MARGIN :, :]], axis=0)
    middle = dot(row_table[...], tile[...]).astype(bf16)
    blocks = [
        dot(strips, inner_table[...]).astype(bf16),
        dot(strips[:, middle_of:], edge_table[middle_of:, :]).astype(bf16),
        dot(strips[:, :middle_of], edge_table[:middle_of, :]).astype(bf16),
    ]
    for at, first in ((0, 0), (1, core - MARGIN)):
        for lanes in range(3):
            rows_out[at, lanes] = blocks[lanes][at * MARGIN : (at + 1) * MARGIN]
        strip = middle[:, first : first + MARGIN]
        side_out[at] = jnp.concatenate([strip[:band], strip[band:]], axis=1)
    peers = n_cond - 1
    for _, _, flag, _ in around:
        peers = peers + jnp.where(flag & sender, n_cond, 0)
    pl.semaphore_wait(barrier, peers)

    def halo(i, q):
        down, right, flag, there = around[i]
        outgoing, incoming = (rows_out, rows_in) if down else (side_out, side_in)
        return pltpu.make_async_remote_copy(
            src_ref=outgoing.at[slot(down, right)],
            dst_ref=incoming.at[slot(-down, -right)],
            send_sem=halo_send.at[q, i],
            recv_sem=halo_recv.at[len(around) - 1 - i],
            device_id={"tile": there, "cond": q},
        )

    for q in range(n_cond):
        for i in range(len(around)):

            @pl.when(around[i][2] & sender)
            def _():
                halo(i, q).start()

    for load in loads[2:]:
        load.wait()
    inner = dot(middle, inner_table[...])
    tops = []
    for c in range(conds):
        weight_sum = weight[c, 0]
        for k in range(1, kerns):
            weight_sum = weight_sum + weight[c, k]
        gain = jnp.full((8, grid), steepness * dose[c], f32) / jnp.full((8, grid), weight_sum, f32)
        tops.append(steepness * threshold[c])
        for k in range(kerns):
            root = jnp.sqrt(gain * weight[c, k])
            scaled = kern[c, k].astype(f32) * root[0:1]
            plain[c, k] = scaled
            turned[c, k] = pltpu.roll(scaled, band, 1)

    for i in range(len(around)):

        @pl.when(around[i][2])
        def _():
            halo(len(around) - 1 - i, 0).wait_recv()

    outer = rows_in[...].astype(f32)
    outer = (outer[:, 0] + outer[:, 1] + outer[:, 2]).reshape(2 * MARGIN, 2 * band).astype(bf16)
    sides = dot(jnp.concatenate([side_in[0], side_in[1]], axis=1), side_table[...])
    sides = jnp.concatenate([sides[:, : 2 * band], sides[:, 2 * band :]], axis=0)
    quarters = inner + dot(outer_rows[:, : 2 * MARGIN], outer) + sides
    quarters = quarters * (1.0 / ((core + 2 * MARGIN) * band))
    turned_quarters = pltpu.roll(quarters, band, 1)
    lane = lax.broadcasted_iota(jnp.int32, (band, 2 * band), 1)
    first = lane < band
    top, bottom = quarters[:band], quarters[band:]
    top_turned, bottom_turned = turned_quarters[:band], turned_quarters[band:]
    spec_same = jnp.where(first, top + bottom_turned, top_turned + bottom)
    spec_cross = jnp.where(first, top_turned - bottom, bottom_turned - top)

    bunches = [list(range(max(conds - 2, 0)))] + [[c] for c in range(max(conds - 2, 0), conds)]
    bunches = [bunch for bunch in bunches if bunch]

    def swap(i, step):
        chosen = pl.ds(bunches[i][0], len(bunches[i]))
        return pltpu.make_async_remote_copy(
            src_ref=level.at[chosen],
            dst_ref=arrived.at[step - 1, chosen],
            send_sem=swap_send.at[step - 1, i],
            recv_sem=swap_recv.at[step - 1, i],
            device_id={"cond": lax.rem(me + step, n_cond)},
        )

    def halves(c, start, size):
        prod = [
            (spec_same * plain[c, k] + spec_cross * turned[c, k]).astype(bf16)
            for k in range(start, start + size)
        ]
        half = dot(jnp.concatenate(prod, axis=0), half_table[...]).astype(bf16)
        return [half[j * band : (j + 1) * band] for j in range(size)]

    def powers(total, pair):
        stacked = jnp.concatenate(
            [
                jnp.concatenate([h[:, :grid] for h in pair], axis=1),
                jnp.concatenate([h[:, grid:] for h in pair], axis=1),
            ],
            axis=0,
        )
        sampling = jnp.concatenate([field_table[:, :grid], field_table[:, grid:]], axis=0)
        field = dot(sampling, stacked)
        power = field[:grid] * field[:grid] + field[grid:] * field[grid:]
        for j in range(len(pair)):
            total = total + power[:, j * grid : (j + 1) * grid]
        return total

    groups = [
        (c, start, min(GROUP, kerns - start)) for c in range(conds) for start in range(0, kerns, GROUP)
    ]
    ready = [halves(*groups[i]) for i in range(min(AHEAD, len(groups)))]
    total = None
    due = []
    for i, (c, start, size) in enumerate(groups):
        if i + AHEAD < len(groups):
            ready.append(halves(*groups[i + AHEAD]))
        if start == 0:
            total = jnp.full((grid, grid), -tops[c], f32)
        half = ready[i]
        for j in range(0, size, 2):
            total = powers(total, half[j : j + 2])
        if start + size == kerns:
            level[c] = total
            for number, bunch in enumerate(bunches):
                if c == bunch[-1]:
                    due.append((i + DELAY, number))
        while due and (due[0][0] <= i or i + 1 == len(groups)):
            number = due.pop(0)[1]
            for step in range(1, n_cond):
                swap(number, step).start()

    share = high_out.shape[1]
    row_part = rise_rows[pl.ds(pl.multiple_of(me * share, share), share), :]
    row_part = jnp.concatenate([row_part[:, :grid], row_part], axis=1)
    col_part = jnp.concatenate([rise_cols[:grid], rise_cols[...]], axis=0)

    def include(bounds, values):
        high, low = high_low(jnp.concatenate(values, axis=1))
        wide = dot(row_part, jnp.concatenate([high, low, high], axis=0))
        wide = jnp.concatenate([wide[:, j * grid : (j + 1) * grid] for j in range(len(values))], axis=0)
        high, low = high_low(wide)
        blurred = dot(jnp.concatenate([high, low, high], axis=1), col_part)
        for j in range(len(values)):
            one = blurred[j * share : (j + 1) * share]
            bounds = (one, one) if bounds is None else (
                jnp.maximum(bounds[0], one),
                jnp.minimum(bounds[1], one),
            )
        return bounds

    def theirs(numbers):
        found = []
        for number in numbers:
            for step in range(1, n_cond):
                swap(number, step).wait_recv()
                found += [arrived[step - 1, c] for c in bunches[number]]
        return found

    early = theirs(range(len(bunches) - 2))
    bounds = include(None, [level[c] for c in range(conds)] + early)
    bounds = include(bounds, theirs(range(max(len(bunches) - 2, 0), len(bunches))))
    high_out[0] = bounds[0]
    low_out[0] = bounds[1]
    for step in range(1, n_cond):
        for number in range(len(bunches)):
            swap(number, step).wait_send()
    for q in range(n_cond):
        for i in range(len(around)):

            @pl.when(around[i][2] & sender)
            def _():
                halo(i, q).wait_send()


def on_device(mask, kernels, socs_weight, dose, threshold):
    core = mask.shape[1]
    conds, kerns, band, _ = kernels.shape
    n_cond = lax.axis_size("cond")
    first_table, later_table, parts = make_tables(core, band)
    share = core // n_cond
    anywhere = pl.BlockSpec(memory_space=pl.ANY)
    vmem = pl.BlockSpec(memory_space=pltpu.VMEM)
    grid = 2 * band
    out = pltpu.VMEM((1, share, core), f32)
    high, low = pl.pallas_call(
        functools.partial(body, parts),
        out_shape=(out, out),
        in_specs=[anywhere] * 7,
        out_specs=(vmem, vmem),
        scratch_shapes=[
            pltpu.SMEM(socs_weight.shape, f32),
            pltpu.SMEM(dose.shape, f32),
            pltpu.SMEM(threshold.shape, f32),
            pltpu.VMEM((core, core), bf16),
            pltpu.VMEM(kernels.shape, bf16),
            pltpu.VMEM(first_table.shape, bf16),
            pltpu.VMEM(later_table.shape, bf16),
            pltpu.VMEM((2, 3, MARGIN, 2 * band), bf16),
            pltpu.VMEM((2, 3, MARGIN, 2 * band), bf16),
            pltpu.VMEM((2, band, 2 * MARGIN), bf16),
            pltpu.VMEM((2, band, 2 * MARGIN), bf16),
            pltpu.VMEM((conds, grid, grid), f32),
            pltpu.VMEM((n_cond - 1, conds, grid, grid), f32),
            pltpu.SemaphoreType.DMA((7,)),
            pltpu.SemaphoreType.DMA((n_cond, 8)),
            pltpu.SemaphoreType.DMA((8,)),
            pltpu.SemaphoreType.DMA((n_cond - 1, min(conds, 3))),
            pltpu.SemaphoreType.DMA((n_cond - 1, min(conds, 3))),
            pltpu.VMEM(kernels.shape, f32),
            pltpu.VMEM(kernels.shape, f32),
        ],
        compiler_params=pltpu.CompilerParams(collective_id=0, has_side_effects=True),
    )(mask, kernels, socs_weight, dose, threshold, jnp.asarray(first_table), jnp.asarray(later_table))
    return jax.nn.sigmoid(high), jax.nn.sigmoid(low)


def solution(mesh):
    return jax.shard_map(
        on_device,
        mesh=mesh,
        in_specs=(
            P(("parts", "tile"), None, None),
            P("cond", None, None, None),
            P("cond", None),
            P("cond"),
            P("cond"),
        ),
        out_specs=(P(("parts", "tile"), "cond", None), P(("parts", "tile"), "cond", None)),
        check_vma=False,
    )
```

time: 16.2 us -> 14.9 us (0.920)
  Pallas kernels: 14.6 us -> 13.3 us
    pallas_call x1, Pallas kernels: 14.6 us -> 13.3 us  [on_device(): pl.pallas_call(functools.partial(body, parts), out_shape=(out, out), in_s...]
where the time goes in v2:
time: 14.9 us; the launch traced here: 14.7 us
  Pallas kernels  13.3 us (89%)
  other arithmetic  0.77 us (5%)
  between operations  0.64 us (4%)
    pallas_call x1, Pallas kernels, on_device(): pl.pallas_call(functools.partial(body, parts), out_shape=(out, out), in_s...  13.3 us
    div x1, other arithmetic, on_device(): return (jax.nn.sigmoid(high), jax.nn.sigmoid(low))  0.77 us

profile of v2, /device:TPU:0, one launch (start us, length us, event | category | flops | bytes accessed | tf_op | source)
XLA Modules:
  0.0 14.7 jit_solution(5912418013431328659)
XLA Ops:
  0.6 13.3 %shard_map.86 = (f32[1,128,256]{2,1,0:T(8,128)S(1)}, f32[1,128,256]{2,1,0:T(8,128)S(1)}) custom-call(bf16[1,256,256]{2,1,0:T(8,128)(2,1)} %mask_hbm.1, bf16[4,24,64,128]{3,2,1,0:T(8,128)(2,1)} %kern_hbm.1, f32[4,24]{1,0:T(4,128)} %weight_hbm.1, f32[4]{0:T(128)} %dose_hbm.1, f32[4]{0:T(128)} %threshold_hbm.1, bf16[384,256]{1,0:T(8,128)(2,1)} %constant.6.clone.first_hbm, ...), custom_call_target="tpu_custom_call" | custom-call | tf_op jit(solution)/shard_map/pallas_call | solution.py:378
  14.0 0.8 %add_divide_fusion = (f32[1,128,256]{2,1,0:T(8,128)}, f32[1,128,256]{2,1,0:T(8,128)}) fusion(f32[1,128,256]{2,1,0:T(8,128)S(1)} %get-tuple-element.5, f32[1,128,256]{2,1,0:T(8,128)S(1)} %get-tuple-element.4), kind=kLoop, calls=%fused_computation | loop fusion | flops 196608 | bytes 524288 | tf_op jit(solution)/shard_map/div | solution.py:407

commit v3 on v2

--- a/solution.py
+++ b/solution.py
@@ -14,6 +14,8 @@
 GROUP = 4
 AHEAD = 2
 DELAY = 2
+PIECES = 4
+ORDER = (1, 4, 0, 2, 3, 6, 5, 7)
 
 diffusion = 2.0
 steepness = 8.0
@@ -105,6 +107,14 @@
     return jnp.dot(a, b, preferred_element_type=f32)
 
 
+def start_split(load):
+    src, dst, sem = load
+    rows = dst.shape[0] // PIECES
+    for n in range(PIECES):
+        piece = pl.ds(n * rows, rows)
+        pltpu.make_async_copy(src.at[piece], dst.at[piece], sem).start()
+
+
 def body(
     parts,
     mask_hbm,
@@ -129,13 +139,13 @@
     side_in,
     level,
     arrived,
-    load_sem,
-    halo_send,
     halo_recv,
-    swap_send,
     swap_recv,
     plain,
     turned,
+    load_sem,
+    halo_send,
+    swap_send,
 ):
     core = mask_hbm.shape[1]
     conds, kerns, band, _ = kern_hbm.shape
@@ -154,7 +164,7 @@
     edge_table = first_table.at[pl.ds(grid, core), pl.ds(grid, grid)]
 
     loads = [
-        pltpu.make_async_copy(src, dst, load_sem.at[i])
+        (src, dst, load_sem.at[i])
         for i, (src, dst) in enumerate(
             (
                 (mask_hbm.at[0], tile),
@@ -168,7 +178,7 @@
         )
     ]
     for load in loads[:2]:
-        load.start()
+        start_split(load)
 
     barrier = pltpu.get_barrier_semaphore()
     for _, _, flag, there in around:
@@ -188,9 +198,9 @@
             buffer[at] = jnp.zeros(buffer.shape[len(at) :], bf16)
 
     for load in loads[:2]:
-        load.wait()
+        pltpu.make_async_copy(*load).wait()
     for load in loads[2:]:
-        load.start()
+        pltpu.make_async_copy(*load).start()
     strips = jnp.concatenate([tile[:MARGIN, :], tile[core - MARGIN :, :]], axis=0)
     middle = dot(row_table[...], tile[...]).astype(bf16)
     blocks = [
@@ -219,15 +229,15 @@
             device_id={"tile": there, "cond": q},
         )
 
-    for q in range(n_cond):
-        for i in range(len(around)):
-
-            @pl.when(around[i][2] & sender)
-            def _():
+    for i in ORDER:
+
+        @pl.when(around[i][2] & sender)
+        def _():
+            for q in range(n_cond):
                 halo(i, q).start()
 
     for load in loads[2:]:
-        load.wait()
+        pltpu.make_async_copy(*load).wait()
     inner = dot(middle, inner_table[...])
     tops = []
     for c in range(conds):
@@ -241,6 +251,13 @@
             scaled = kern[c, k].astype(f32) * root[0:1]
             plain[c, k] = scaled
             turned[c, k] = pltpu.roll(scaled, band, 1)
+
+    for i in ORDER:
+
+        @pl.when(around[i][2] & sender)
+        def _():
+            for q in range(n_cond):
+                halo(i, q).wait_send()
 
     for i in range(len(around)):
 
@@ -357,12 +374,6 @@
     for step in range(1, n_cond):
         for number in range(len(bunches)):
             swap(number, step).wait_send()
-    for q in range(n_cond):
-        for i in range(len(around)):
-
-            @pl.when(around[i][2] & sender)
-            def _():
-                halo(i, q).wait_send()
 
 
 def on_device(mask, kernels, socs_weight, dose, threshold):
@@ -375,8 +386,17 @@
     vmem = pl.BlockSpec(memory_space=pltpu.VMEM)
     grid = 2 * band
     out = pltpu.VMEM((1, share, core), f32)
+
+    def scoped(*refs):
+        pl.run_scoped(
+            functools.partial(body, parts, *refs),
+            pltpu.SemaphoreType.DMA((7,)),
+            pltpu.SemaphoreType.DMA((n_cond, 8)),
+            pltpu.SemaphoreType.DMA((n_cond - 1, min(conds, 3))),
+        )
+
     high, low = pl.pallas_call(
-        functools.partial(body, parts),
+        scoped,
         out_shape=(out, out),
         in_specs=[anywhere] * 7,
         out_specs=(vmem, vmem),
@@ -394,10 +414,7 @@
             pltpu.VMEM((2, band, 2 * MARGIN), bf16),
             pltpu.VMEM((conds, grid, grid), f32),
             pltpu.VMEM((n_cond - 1, conds, grid, grid), f32),
-            pltpu.SemaphoreType.DMA((7,)),
-            pltpu.SemaphoreType.DMA((n_cond, 8)),
             pltpu.SemaphoreType.DMA((8,)),
-            pltpu.SemaphoreType.DMA((n_cond - 1, min(conds, 3))),
             pltpu.SemaphoreType.DMA((n_cond - 1, min(conds, 3))),
             pltpu.VMEM(kernels.shape, f32),
             pltpu.VMEM(kernels.shape, f32),

time: 14.9 us -> 14.5 us (0.973)
  Pallas kernels: 13.3 us -> 12.9 us
    pallas_call x1, Pallas kernels: 13.3 us -> 12.9 us  [on_device(): pl.pallas_call(scoped, out_shape=(out, out), in_specs=[anywhere] * 7, out...]
where the time goes in v3:
time: 14.5 us; the launch traced here: 14.3 us
  Pallas kernels  12.9 us (89%)
  other arithmetic  0.77 us (5%)
  between operations  0.64 us (4%)
    pallas_call x1, Pallas kernels, on_device(): pl.pallas_call(scoped, out_shape=(out, out), in_specs=[anywhere] * 7, out...  12.9 us
    div x1, other arithmetic, on_device(): return (jax.nn.sigmoid(high), jax.nn.sigmoid(low))  0.77 us

profile of v3, /device:TPU:0, one launch (start us, length us, event | category | flops | bytes accessed | tf_op | source)
XLA Modules:
  0.0 14.3 jit_solution(16176464700251545942)
XLA Ops:
  0.6 12.9 %shard_map.86 = (f32[1,128,256]{2,1,0:T(8,128)S(1)}, f32[1,128,256]{2,1,0:T(8,128)S(1)}) custom-call(bf16[1,256,256]{2,1,0:T(8,128)(2,1)} %refs_0_.1, bf16[4,24,64,128]{3,2,1,0:T(8,128)(2,1)} %refs_1_.1, f32[4,24]{1,0:T(4,128)} %refs_2_.1, f32[4]{0:T(128)} %refs_3_.1, f32[4]{0:T(128)} %refs_4_.1, bf16[384,256]{1,0:T(8,128)(2,1)} %constant.6.clone.refs_5_, ...), custom_call_target="tpu_custom_call" | custom-call | tf_op jit(solution)/shard_map/pallas_call | solution.py:398
  13.5 0.8 %add_divide_fusion = (f32[1,128,256]{2,1,0:T(8,128)}, f32[1,128,256]{2,1,0:T(8,128)}) fusion(f32[1,128,256]{2,1,0:T(8,128)S(1)} %get-tuple-element.5, f32[1,128,256]{2,1,0:T(8,128)S(1)} %get-tuple-element.4), kind=kLoop, calls=%fused_computation | loop fusion | flops 196608 | bytes 524288 | tf_op jit(solution)/shard_map/div | solution.py:424

commit v4 on v3

--- a/solution.py
+++ b/solution.py
@@ -14,7 +14,8 @@
 GROUP = 4
 AHEAD = 2
 DELAY = 2
-PIECES = 4
+PIECES = 8
+WRITES = 8
 ORDER = (1, 4, 0, 2, 3, 6, 5, 7)
 
 diffusion = 2.0
@@ -154,8 +155,10 @@
     n_cond = lax.axis_size("cond")
     me = lax.axis_index("cond")
     near = n_cond - 1
-    sender = me == near
     around = neighbours()
+    tiles = lax.axis_size("tile")
+    sends = [flag & jnp.where(there <= tiles // 2, me == near, me == 0) for _, _, flag, there in around]
+    caller = jnp.where(lax.axis_index("tile") <= tiles // 2, near, 0)
     side_table, half_table, field_table, outer_rows, rise_cols, rise_rows = (
         later_table.at[pl.ds(lo, hi - lo)] for lo, hi in zip(parts[:-1], parts[1:])
     )
@@ -181,11 +184,12 @@
         start_split(load)
 
     barrier = pltpu.get_barrier_semaphore()
-    for _, _, flag, there in around:
+    for i in reversed(range(len(around))):
+        _, _, flag, there = around[i]
 
         @pl.when(flag)
         def _():
-            pl.semaphore_signal(barrier, inc=1, device_id={"tile": there, "cond": near})
+            pl.semaphore_signal(barrier, inc=1, device_id={"tile": there, "cond": caller})
 
     for step in range(1, n_cond):
         pl.semaphore_signal(barrier, inc=1, device_id={"cond": lax.rem(me + step, n_cond)})
@@ -214,12 +218,12 @@
         strip = middle[:, first : first + MARGIN]
         side_out[at] = jnp.concatenate([strip[:band], strip[band:]], axis=1)
     peers = n_cond - 1
-    for _, _, flag, _ in around:
-        peers = peers + jnp.where(flag & sender, n_cond, 0)
+    for send in sends:
+        peers = peers + jnp.where(send, n_cond, 0)
     pl.semaphore_wait(barrier, peers)
 
     def halo(i, q):
-        down, right, flag, there = around[i]
+        down, right, _, there = around[i]
         outgoing, incoming = (rows_out, rows_in) if down else (side_out, side_in)
         return pltpu.make_async_remote_copy(
             src_ref=outgoing.at[slot(down, right)],
@@ -231,7 +235,7 @@
 
     for i in ORDER:
 
-        @pl.when(around[i][2] & sender)
+        @pl.when(sends[i])
         def _():
             for q in range(n_cond):
                 halo(i, q).start()
@@ -254,7 +258,7 @@
 
     for i in ORDER:
 
-        @pl.when(around[i][2] & sender)
+        @pl.when(sends[i])
         def _():
             for q in range(n_cond):
                 halo(i, q).wait_send()
@@ -374,6 +378,27 @@
     for step in range(1, n_cond):
         for number in range(len(bunches)):
             swap(number, step).wait_send()
+
+
+def finish(high, low, high_out, low_out, staged):
+    rows = high.shape[1] // WRITES
+
+    def write(sem):
+        copies = []
+        for n in range(WRITES):
+            piece = pl.ds(n * rows, rows)
+            for which, (src, dst) in enumerate(((high, high_out), (low, low_out))):
+                staged[which, piece] = jax.nn.sigmoid(src[0, piece])
+                copies.append(
+                    pltpu.make_async_copy(
+                        staged.at[which, piece], dst.at[0, piece], sem.at[which, n]
+                    )
+                )
+                copies[-1].start()
+        for copy in copies:
+            copy.wait()
+
+    pl.run_scoped(write, pltpu.SemaphoreType.DMA((2, WRITES)))
 
 
 def on_device(mask, kernels, socs_weight, dose, threshold):
@@ -421,7 +446,14 @@
         ],
         compiler_params=pltpu.CompilerParams(collective_id=0, has_side_effects=True),
     )(mask, kernels, socs_weight, dose, threshold, jnp.asarray(first_table), jnp.asarray(later_table))
-    return jax.nn.sigmoid(high), jax.nn.sigmoid(low)
+    out = jax.ShapeDtypeStruct((1, share, core), f32)
+    return pl.pallas_call(
+        finish,
+        out_shape=(out, out),
+        in_specs=[vmem] * 2,
+        out_specs=(anywhere, anywhere),
+        scratch_shapes=[pltpu.VMEM((2, share, core), f32)],
+    )(*(pltpu.with_memory_space_constraint(x, pltpu.VMEM) for x in (high, low)))
 
 
 def solution(mesh):

time: 14.5 us -> 14.1 us (0.972)
  other arithmetic: 0.77 us -> 0 us
  Pallas kernels: 12.9 us -> 13.2 us
    div x1 -> x0, other arithmetic: 0.77 us -> none  [on_device(): return (jax.nn.sigmoid(high), jax.nn.sigmoid(low))]
    pallas_call x0 -> x1, Pallas kernels: none -> 0.7 us  [on_device(): pl.pallas_call(finish, out_shape=(out, out), in_specs=[vmem] * 2, out_spe...]
    pallas_call x1, Pallas kernels: 12.9 us -> 12.5 us  [on_device(): pl.pallas_call(scoped, out_shape=(out, out), in_specs=[anywhere] * 7, out...]
where the time goes in v4:
time: 14.1 us; the launch traced here: 13.9 us
  Pallas kernels  13.2 us (94%)
  between operations  0.64 us (5%)
    pallas_call x1, Pallas kernels, on_device(): pl.pallas_call(scoped, out_shape=(out, out), in_specs=[anywhere] * 7, out...  12.5 us
    pallas_call x1, Pallas kernels, on_device(): pl.pallas_call(finish, out_shape=(out, out), in_specs=[vmem] * 2, out_spe...  0.7 us

profile of v4, /device:TPU:0, one launch (start us, length us, event | category | flops | bytes accessed | tf_op | source)
XLA Modules:
  0.0 13.9 jit_solution(18269785884723687745)
XLA Ops:
  0.6 12.5 %shard_map.86 = (f32[1,128,256]{2,1,0:T(8,128)S(1)}, f32[1,128,256]{2,1,0:T(8,128)S(1)}) custom-call(bf16[1,256,256]{2,1,0:T(8,128)(2,1)} %refs_0_.1, bf16[4,24,64,128]{3,2,1,0:T(8,128)(2,1)} %refs_1_.1, f32[4,24]{1,0:T(4,128)} %refs_2_.1, f32[4]{0:T(128)} %refs_3_.1, f32[4]{0:T(128)} %refs_4_.1, bf16[384,256]{1,0:T(8,128)(2,1)} %constant.4.clone.refs_5_, ...), custom_call_target="tpu_custom_call" | custom-call | tf_op jit(solution)/shard_map/pallas_call | solution.py:423
  13.2 0.7 %shard_map.87 = (f32[1,128,256]{2,1,0:T(8,128)}, f32[1,128,256]{2,1,0:T(8,128)}) custom-call(f32[1,128,256]{2,1,0:T(8,128)S(1)} %get-tuple-element.4.high, f32[1,128,256]{2,1,0:T(8,128)S(1)} %get-tuple-element.5.low), custom_call_target="tpu_custom_call" | custom-call | tf_op jit(solution)/shard_map/pallas_call | solution.py:450

commit v5 on v4

--- a/solution.py
+++ b/solution.py
@@ -16,6 +16,7 @@
 DELAY = 2
 PIECES = 8
 WRITES = 8
+SWAPS = 1
 ORDER = (1, 4, 0, 2, 3, 6, 5, 7)
 
 diffusion = 2.0
@@ -44,13 +45,17 @@
     row_table = np.concatenate([cos_in[order].T, -sin_in[order].T], axis=0)
     both = np.concatenate([cos_in, sin_in], axis=1)
     left, inner, right = both[:MARGIN], both[MARGIN : MARGIN + core], both[MARGIN + core :]
-    zero = np.zeros_like(left)
     gap = np.zeros((core - 2 * MARGIN, 2 * band))
     edges = np.concatenate([right, gap, left], axis=0)
     first_table = np.concatenate(
         [row_table[:, :core], np.concatenate([inner, edges], axis=1)], axis=0
     )
-    side_table = np.block([[left, zero], [zero, left], [right, zero], [zero, right]])
+    strips = []
+    for strip in (left, right):
+        cos, sin = strip[:, :band], strip[:, band:]
+        strips.append(np.concatenate([cos, cos, sin, -sin], axis=1))
+        strips.append(np.concatenate([sin, sin, -cos, cos], axis=1))
+    side_table = np.concatenate(strips, axis=0)
     cos_grid, sin_grid = trig(np.arange(grid)[:, None] * freq[None, :], grid)
     half_table = np.block([[cos_grid.T, sin_grid.T], [-sin_grid.T, cos_grid.T]])
     field_table = np.concatenate(
@@ -151,14 +156,6 @@
     core = mask_hbm.shape[1]
     conds, kerns, band, _ = kern_hbm.shape
     grid = 2 * band
-    middle_of = core // 2
-    n_cond = lax.axis_size("cond")
-    me = lax.axis_index("cond")
-    near = n_cond - 1
-    around = neighbours()
-    tiles = lax.axis_size("tile")
-    sends = [flag & jnp.where(there <= tiles // 2, me == near, me == 0) for _, _, flag, there in around]
-    caller = jnp.where(lax.axis_index("tile") <= tiles // 2, near, 0)
     side_table, half_table, field_table, outer_rows, rise_cols, rise_rows = (
         later_table.at[pl.ds(lo, hi - lo)] for lo, hi in zip(parts[:-1], parts[1:])
     )
@@ -171,7 +168,8 @@
         for i, (src, dst) in enumerate(
             (
                 (mask_hbm.at[0], tile),
-                (first_hbm, first_table),
+                (first_hbm.at[pl.ds(0, grid)], first_table.at[pl.ds(0, grid)]),
+                (first_hbm.at[pl.ds(grid, core)], first_table.at[pl.ds(grid, core)]),
                 (kern_hbm, kern),
                 (weight_hbm, weight),
                 (dose_hbm, dose),
@@ -180,9 +178,17 @@
             )
         )
     ]
-    for load in loads[:2]:
+    for load in loads[:3]:
         start_split(load)
 
+    middle_of = core // 2
+    n_cond = lax.axis_size("cond")
+    me = lax.axis_index("cond")
+    near = n_cond - 1
+    around = neighbours()
+    tiles = lax.axis_size("tile")
+    sends = [flag & jnp.where(there <= tiles // 2 + 1, me == near, me == 0) for _, _, flag, there in around]
+    caller = jnp.where(lax.axis_index("tile") <= tiles // 2 + 1, near, 0)
     barrier = pltpu.get_barrier_semaphore()
     for i in reversed(range(len(around))):
         _, _, flag, there = around[i]
@@ -203,20 +209,16 @@
 
     for load in loads[:2]:
         pltpu.make_async_copy(*load).wait()
-    for load in loads[2:]:
+    for load in loads[3:]:
         pltpu.make_async_copy(*load).start()
-    strips = jnp.concatenate([tile[:MARGIN, :], tile[core - MARGIN :, :]], axis=0)
-    middle = dot(row_table[...], tile[...]).astype(bf16)
-    blocks = [
-        dot(strips, inner_table[...]).astype(bf16),
-        dot(strips[:, middle_of:], edge_table[middle_of:, :]).astype(bf16),
-        dot(strips[:, :middle_of], edge_table[:middle_of, :]).astype(bf16),
-    ]
-    for at, first in ((0, 0), (1, core - MARGIN)):
-        for lanes in range(3):
-            rows_out[at, lanes] = blocks[lanes][at * MARGIN : (at + 1) * MARGIN]
-        strip = middle[:, first : first + MARGIN]
-        side_out[at] = jnp.concatenate([strip[:band], strip[band:]], axis=1)
+    lane = lax.broadcasted_iota(jnp.int32, (band, 2 * band), 1)
+    first = lane < band
+    wide_first = lax.broadcasted_iota(jnp.int32, (core, grid), 1) < band
+    edges = jnp.where(wide_first, tile[:, :grid], tile[:, core - grid :])
+    edges = dot(row_table[...], edges)
+    turned_edges = pltpu.roll(edges, band, 1)
+    side_out[0] = jnp.where(first, edges[:band], turned_edges[band:]).astype(bf16)
+    side_out[1] = jnp.where(first, turned_edges[:band], edges[band:]).astype(bf16)
     peers = n_cond - 1
     for send in sends:
         peers = peers + jnp.where(send, n_cond, 0)
@@ -233,15 +235,30 @@
             device_id={"tile": there, "cond": q},
         )
 
-    for i in ORDER:
-
-        @pl.when(sends[i])
-        def _():
-            for q in range(n_cond):
-                halo(i, q).start()
-
-    for load in loads[2:]:
+    def depart(numbers):
+        for i in numbers:
+
+            @pl.when(sends[i])
+            def _():
+                for q in range(n_cond):
+                    halo(i, q).start()
+
+    depart(i for i in ORDER if not around[i][0])
+    pltpu.make_async_copy(*loads[2]).wait()
+    strips = jnp.concatenate([tile[:MARGIN, :], tile[core - MARGIN :, :]], axis=0)
+    blocks = [
+        dot(strips, inner_table[...]).astype(bf16),
+        dot(strips[:, middle_of:], edge_table[middle_of:, :]).astype(bf16),
+        dot(strips[:, :middle_of], edge_table[:middle_of, :]).astype(bf16),
+    ]
+    for at in range(2):
+        for lanes in range(3):
+            rows_out[at, lanes] = blocks[lanes][at * MARGIN : (at + 1) * MARGIN]
+    depart(i for i in ORDER if around[i][0])
+
+    for load in loads[3:]:
         pltpu.make_async_copy(*load).wait()
+    middle = dot(row_table[...], tile[...]).astype(bf16)
     inner = dot(middle, inner_table[...])
     tops = []
     for c in range(conds):
@@ -251,46 +268,40 @@
         gain = jnp.full((8, grid), steepness * dose[c], f32) / jnp.full((8, grid), weight_sum, f32)
         tops.append(steepness * threshold[c])
         for k in range(kerns):
-            root = jnp.sqrt(gain * weight[c, k])
+            root = jnp.sqrt(gain * weight[c, k]) * (1.0 / ((core + 2 * MARGIN) * band))
             scaled = kern[c, k].astype(f32) * root[0:1]
             plain[c, k] = scaled
             turned[c, k] = pltpu.roll(scaled, band, 1)
 
-    for i in ORDER:
-
-        @pl.when(sends[i])
-        def _():
-            for q in range(n_cond):
-                halo(i, q).wait_send()
-
-    for i in range(len(around)):
-
-        @pl.when(around[i][2])
-        def _():
-            halo(len(around) - 1 - i, 0).wait_recv()
-
+    def arrive(numbers):
+        for i in numbers:
+
+            @pl.when(around[i][2])
+            def _():
+                halo(len(around) - 1 - i, 0).wait_recv()
+
+    arrive(i for i in range(len(around)) if around[i][0])
     outer = rows_in[...].astype(f32)
     outer = (outer[:, 0] + outer[:, 1] + outer[:, 2]).reshape(2 * MARGIN, 2 * band).astype(bf16)
-    sides = dot(jnp.concatenate([side_in[0], side_in[1]], axis=1), side_table[...])
-    sides = jnp.concatenate([sides[:, : 2 * band], sides[:, 2 * band :]], axis=0)
-    quarters = inner + dot(outer_rows[:, : 2 * MARGIN], outer) + sides
-    quarters = quarters * (1.0 / ((core + 2 * MARGIN) * band))
+    quarters = inner + dot(outer_rows[:, : 2 * MARGIN], outer)
     turned_quarters = pltpu.roll(quarters, band, 1)
-    lane = lax.broadcasted_iota(jnp.int32, (band, 2 * band), 1)
-    first = lane < band
     top, bottom = quarters[:band], quarters[band:]
     top_turned, bottom_turned = turned_quarters[:band], turned_quarters[band:]
     spec_same = jnp.where(first, top + bottom_turned, top_turned + bottom)
     spec_cross = jnp.where(first, top_turned - bottom, bottom_turned - top)
+    arrive(i for i in range(len(around)) if not around[i][0])
+    sides = dot(jnp.concatenate([side_in[0], side_in[1]], axis=1), side_table[...])
+    spec_same = spec_same + sides[:, : 2 * band]
+    spec_cross = spec_cross + sides[:, 2 * band :]
 
     bunches = [list(range(max(conds - 2, 0)))] + [[c] for c in range(max(conds - 2, 0), conds)]
     bunches = [bunch for bunch in bunches if bunch]
 
-    def swap(i, step):
+    def swap(i, step, rows=pl.ds(0, grid)):
         chosen = pl.ds(bunches[i][0], len(bunches[i]))
         return pltpu.make_async_remote_copy(
-            src_ref=level.at[chosen],
-            dst_ref=arrived.at[step - 1, chosen],
+            src_ref=level.at[chosen, rows],
+            dst_ref=arrived.at[step - 1, chosen, rows],
             send_sem=swap_send.at[step - 1, i],
             recv_sem=swap_recv.at[step - 1, i],
             device_id={"cond": lax.rem(me + step, n_cond)},
@@ -341,7 +352,8 @@
         while due and (due[0][0] <= i or i + 1 == len(groups)):
             number = due.pop(0)[1]
             for step in range(1, n_cond):
-                swap(number, step).start()
+                for n in range(SWAPS):
+                    swap(number, step, pl.ds(n * (grid // SWAPS), grid // SWAPS)).start()
 
     share = high_out.shape[1]
     row_part = rise_rows[pl.ds(pl.multiple_of(me * share, share), share), :]
@@ -372,6 +384,13 @@
 
     early = theirs(range(len(bunches) - 2))
     bounds = include(None, [level[c] for c in range(conds)] + early)
+    for i in ORDER:
+
+        @pl.when(sends[i])
+        def _():
+            for q in range(n_cond):
+                halo(i, q).wait_send()
+
     bounds = include(bounds, theirs(range(max(len(bunches) - 2, 0), len(bunches))))
     high_out[0] = bounds[0]
     low_out[0] = bounds[1]
@@ -415,7 +434,7 @@
     def scoped(*refs):
         pl.run_scoped(
             functools.partial(body, parts, *refs),
-            pltpu.SemaphoreType.DMA((7,)),
+            pltpu.SemaphoreType.DMA((8,)),
             pltpu.SemaphoreType.DMA((n_cond, 8)),
             pltpu.SemaphoreType.DMA((n_cond - 1, min(conds, 3))),
         )

time: 14.1 us -> 14 us (level)
  no operation moved by 1% of the time
where the time goes in v5:
time: 14 us; the launch traced here: 13.9 us
  Pallas kernels  13.2 us (94%)
  between operations  0.64 us (5%)
    pallas_call x1, Pallas kernels, on_device(): pl.pallas_call(scoped, out_shape=(out, out), in_specs=[anywhere] * 7, out...  12.5 us
    pallas_call x1, Pallas kernels, on_device(): pl.pallas_call(finish, out_shape=(out, out), in_specs=[vmem] * 2, out_spe...  0.7 us

profile of v5, /device:TPU:0, one launch (start us, length us, event | category | flops | bytes accessed | tf_op | source)
XLA Modules:
  0.0 13.9 jit_solution(3268255652439539582)
XLA Ops:
  0.6 12.5 %shard_map.86 = (f32[1,128,256]{2,1,0:T(8,128)S(1)}, f32[1,128,256]{2,1,0:T(8,128)S(1)}) custom-call(bf16[1,256,256]{2,1,0:T(8,128)(2,1)} %refs_0_.1, bf16[4,24,64,128]{3,2,1,0:T(8,128)(2,1)} %refs_1_.1, f32[4,24]{1,0:T(4,128)} %refs_2_.1, f32[4]{0:T(128)} %refs_3_.1, f32[4]{0:T(128)} %refs_4_.1, bf16[384,256]{1,0:T(8,128)(2,1)} %constant.4.clone.refs_5_, ...), custom_call_target="tpu_custom_call" | custom-call | tf_op jit(solution)/shard_map/pallas_call | solution.py:442
  13.2 0.7 %shard_map.87 = (f32[1,128,256]{2,1,0:T(8,128)}, f32[1,128,256]{2,1,0:T(8,128)}) custom-call(f32[1,128,256]{2,1,0:T(8,128)S(1)} %get-tuple-element.4.high, f32[1,128,256]{2,1,0:T(8,128)S(1)} %get-tuple-element.5.low), custom_call_target="tpu_custom_call" | custom-call | tf_op jit(solution)/shard_map/pallas_call | solution.py:469

commit v6 on v5

--- a/solution.py
+++ b/solution.py
@@ -12,12 +12,12 @@
 MARGIN = 64
 BLUR = 8
 GROUP = 4
-AHEAD = 2
+AHEAD = 3
 DELAY = 2
 PIECES = 8
 WRITES = 8
 SWAPS = 1
-ORDER = (1, 4, 0, 2, 3, 6, 5, 7)
+ORDER = (4, 3, 0, 1, 2, 7, 6, 5)
 
 diffusion = 2.0
 steepness = 8.0
@@ -147,11 +147,15 @@
     arrived,
     halo_recv,
     swap_recv,
+    forward_recv,
+    outer,
+    spec,
     plain,
     turned,
     load_sem,
     halo_send,
     swap_send,
+    forward_send,
 ):
     core = mask_hbm.shape[1]
     conds, kerns, band, _ = kern_hbm.shape
@@ -188,12 +192,16 @@
     around = neighbours()
     tiles = lax.axis_size("tile")
     sends = [flag & jnp.where(there <= tiles // 2 + 1, me == near, me == 0) for _, _, flag, there in around]
+
+    def targets(i):
+        return (near,) if around[i][0] else tuple(range(n_cond))
+
     caller = jnp.where(lax.axis_index("tile") <= tiles // 2 + 1, near, 0)
     barrier = pltpu.get_barrier_semaphore()
     for i in reversed(range(len(around))):
-        _, _, flag, there = around[i]
-
-        @pl.when(flag)
+        down, _, flag, there = around[i]
+
+        @pl.when(flag & (me == near) if down else flag)
         def _():
             pl.semaphore_signal(barrier, inc=1, device_id={"tile": there, "cond": caller})
 
@@ -220,8 +228,8 @@
     side_out[0] = jnp.where(first, edges[:band], turned_edges[band:]).astype(bf16)
     side_out[1] = jnp.where(first, turned_edges[:band], edges[band:]).astype(bf16)
     peers = n_cond - 1
-    for send in sends:
-        peers = peers + jnp.where(send, n_cond, 0)
+    for i, send in enumerate(sends):
+        peers = peers + jnp.where(send, len(targets(i)), 0)
     pl.semaphore_wait(barrier, peers)
 
     def halo(i, q):
@@ -240,7 +248,7 @@
 
             @pl.when(sends[i])
             def _():
-                for q in range(n_cond):
+                for q in targets(i):
                     halo(i, q).start()
 
     depart(i for i in ORDER if not around[i][0])
@@ -280,19 +288,50 @@
             def _():
                 halo(len(around) - 1 - i, 0).wait_recv()
 
-    arrive(i for i in range(len(around)) if around[i][0])
-    outer = rows_in[...].astype(f32)
-    outer = (outer[:, 0] + outer[:, 1] + outer[:, 2]).reshape(2 * MARGIN, 2 * band).astype(bf16)
-    quarters = inner + dot(outer_rows[:, : 2 * MARGIN], outer)
-    turned_quarters = pltpu.roll(quarters, band, 1)
-    top, bottom = quarters[:band], quarters[band:]
-    top_turned, bottom_turned = turned_quarters[:band], turned_quarters[band:]
-    spec_same = jnp.where(first, top + bottom_turned, top_turned + bottom)
-    spec_cross = jnp.where(first, top_turned - bottom, bottom_turned - top)
-    arrive(i for i in range(len(around)) if not around[i][0])
-    sides = dot(jnp.concatenate([side_in[0], side_in[1]], axis=1), side_table[...])
-    spec_same = spec_same + sides[:, : 2 * band]
-    spec_cross = spec_cross + sides[:, 2 * band :]
+    def forward(q):
+        return pltpu.make_async_remote_copy(
+            src_ref=outer,
+            dst_ref=outer,
+            send_sem=forward_send.at[q],
+            recv_sem=forward_recv,
+            device_id={"cond": q},
+        )
+
+    def from_rows():
+        quarters = inner + dot(outer_rows[:, : 2 * MARGIN], outer[...])
+        turned_quarters = pltpu.roll(quarters, band, 1)
+        top, bottom = quarters[:band], quarters[band:]
+        top_turned, bottom_turned = turned_quarters[:band], turned_quarters[band:]
+        same = jnp.where(first, top + bottom_turned, top_turned + bottom)
+        cross = jnp.where(first, top_turned - bottom, bottom_turned - top)
+        return same, cross
+
+    def from_sides(same, cross):
+        sides = dot(jnp.concatenate([side_in[0], side_in[1]], axis=1), side_table[...])
+        spec[0] = same + sides[:, : 2 * band]
+        spec[1] = cross + sides[:, 2 * band :]
+
+    beside = [i for i in range(len(around)) if not around[i][0]]
+
+    @pl.when(me == near)
+    def _():
+        arrive(i for i in range(len(around)) if around[i][0])
+        rows = rows_in[...].astype(f32)
+        rows = rows[:, 0] + rows[:, 1] + rows[:, 2]
+        outer[...] = rows.reshape(2 * MARGIN, 2 * band).astype(bf16)
+        for q in range(near):
+            forward(q).start()
+        same, cross = from_rows()
+        arrive(beside)
+        from_sides(same, cross)
+
+    @pl.when(me != near)
+    def _():
+        arrive(beside)
+        forward(0).wait_recv()
+        from_sides(*from_rows())
+
+    spec_same, spec_cross = spec[0], spec[1]
 
     bunches = [list(range(max(conds - 2, 0)))] + [[c] for c in range(max(conds - 2, 0), conds)]
     bunches = [bunch for bunch in bunches if bunch]
@@ -388,8 +427,13 @@
 
         @pl.when(sends[i])
         def _():
-            for q in range(n_cond):
+            for q in targets(i):
                 halo(i, q).wait_send()
+
+    @pl.when(me == near)
+    def _():
+        for q in range(near):
+            forward(q).wait_send()
 
     bounds = include(bounds, theirs(range(max(len(bunches) - 2, 0), len(bunches))))
     high_out[0] = bounds[0]
@@ -437,6 +481,7 @@
             pltpu.SemaphoreType.DMA((8,)),
             pltpu.SemaphoreType.DMA((n_cond, 8)),
             pltpu.SemaphoreType.DMA((n_cond - 1, min(conds, 3))),
+            pltpu.SemaphoreType.DMA((n_cond,)),
         )
 
     high, low = pl.pallas_call(
@@ -460,6 +505,9 @@
             pltpu.VMEM((n_cond - 1, conds, grid, grid), f32),
             pltpu.SemaphoreType.DMA((8,)),
             pltpu.SemaphoreType.DMA((n_cond - 1, min(conds, 3))),
+            pltpu.SemaphoreType.DMA,
+            pltpu.VMEM((2 * MARGIN, 2 * band), bf16),
+            pltpu.VMEM((2, band, 2 * band), f32),
             pltpu.VMEM(kernels.shape, f32),
             pltpu.VMEM(kernels.shape, f32),
         ],

time: 14 us -> 13.8 us (0.986)
  Pallas kernels: 13.2 us -> 13 us
    pallas_call x1, Pallas kernels: 12.5 us -> 12.3 us  [on_device(): pl.pallas_call(scoped, out_shape=(out, out), in_specs=[anywhere] * 7, out...]
where the time goes in v6:
time: 13.8 us; the launch traced here: 13.6 us
  Pallas kernels  13 us (94%)
  between operations  0.64 us (5%)
    pallas_call x1, Pallas kernels, on_device(): pl.pallas_call(scoped, out_shape=(out, out), in_specs=[anywhere] * 7, out...  12.3 us
    pallas_call x1, Pallas kernels, on_device(): pl.pallas_call(finish, out_shape=(out, out), in_specs=[vmem] * 2, out_spe...  0.7 us

profile of v6, /device:TPU:0, one launch (start us, length us, event | category | flops | bytes accessed | tf_op | source)
XLA Modules:
  0.0 13.6 jit_solution(17306338751501131236)
XLA Ops:
  0.6 12.3 %shard_map.86 = (f32[1,128,256]{2,1,0:T(8,128)S(1)}, f32[1,128,256]{2,1,0:T(8,128)S(1)}) custom-call(bf16[1,256,256]{2,1,0:T(8,128)(2,1)} %refs_0_.1, bf16[4,24,64,128]{3,2,1,0:T(8,128)(2,1)} %refs_1_.1, f32[4,24]{1,0:T(4,128)} %refs_2_.1, f32[4]{0:T(128)} %refs_3_.1, f32[4]{0:T(128)} %refs_4_.1, bf16[384,256]{1,0:T(8,128)(2,1)} %constant.4.clone.refs_5_, ...), custom_call_target="tpu_custom_call" | custom-call | tf_op jit(solution)/shard_map/pallas_call | solution.py:487
  12.9 0.7 %shard_map.87 = (f32[1,128,256]{2,1,0:T(8,128)}, f32[1,128,256]{2,1,0:T(8,128)}) custom-call(f32[1,128,256]{2,1,0:T(8,128)S(1)} %get-tuple-element.4.high, f32[1,128,256]{2,1,0:T(8,128)S(1)} %get-tuple-element.5.low), custom_call_target="tpu_custom_call" | custom-call | tf_op jit(solution)/shard_map/pallas_call | solution.py:517

commit v7 on v6

--- a/solution.py
+++ b/solution.py
@@ -182,7 +182,7 @@
             )
         )
     ]
-    for load in loads[:3]:
+    for load in loads[:2]:
         start_split(load)
 
     middle_of = core // 2
@@ -207,6 +207,7 @@
 
     for step in range(1, n_cond):
         pl.semaphore_signal(barrier, inc=1, device_id={"cond": lax.rem(me + step, n_cond)})
+    start_split(loads[2])
     for down, right, flag, _ in around:
 
         @pl.when(jnp.logical_not(flag))
@@ -311,6 +312,14 @@
         spec[0] = same + sides[:, : 2 * band]
         spec[1] = cross + sides[:, 2 * band :]
 
+    def departed():
+        for i in ORDER:
+
+            @pl.when(sends[i])
+            def _():
+                for q in targets(i):
+                    halo(i, q).wait_send()
+
     beside = [i for i in range(len(around)) if not around[i][0]]
 
     @pl.when(me == near)
@@ -328,6 +337,7 @@
     @pl.when(me != near)
     def _():
         arrive(beside)
+        departed()
         forward(0).wait_recv()
         from_sides(*from_rows())
 
@@ -396,21 +406,25 @@
 
     share = high_out.shape[1]
     row_part = rise_rows[pl.ds(pl.multiple_of(me * share, share), share), :]
-    row_part = jnp.concatenate([row_part[:, :grid], row_part], axis=1)
-    col_part = jnp.concatenate([rise_cols[:grid], rise_cols[...]], axis=0)
+    row_part = jnp.concatenate([row_part, row_part[:, :grid]], axis=1)
+    col_part = jnp.concatenate([rise_cols[...], rise_cols[:grid]], axis=0)
 
     def include(bounds, values):
         high, low = high_low(jnp.concatenate(values, axis=1))
-        wide = dot(row_part, jnp.concatenate([high, low, high], axis=0))
-        wide = jnp.concatenate([wide[:, j * grid : (j + 1) * grid] for j in range(len(values))], axis=0)
-        high, low = high_low(wide)
-        blurred = dot(jnp.concatenate([high, low, high], axis=1), col_part)
-        for j in range(len(values)):
-            one = blurred[j * share : (j + 1) * share]
-            bounds = (one, one) if bounds is None else (
-                jnp.maximum(bounds[0], one),
-                jnp.minimum(bounds[1], one),
-            )
+        wide = dot(row_part, jnp.concatenate([high, high, low], axis=0))
+        half = (len(values) + 1) // 2
+        for some in (range(half), range(half, len(values))):
+            if not len(some):
+                continue
+            part = jnp.concatenate([wide[:, j * grid : (j + 1) * grid] for j in some], axis=0)
+            high, low = high_low(part)
+            blurred = dot(jnp.concatenate([high, high, low], axis=1), col_part)
+            for j in range(len(some)):
+                one = blurred[j * share : (j + 1) * share]
+                bounds = (one, one) if bounds is None else (
+                    jnp.maximum(bounds[0], one),
+                    jnp.minimum(bounds[1], one),
+                )
         return bounds
 
     def theirs(numbers):
@@ -423,15 +437,9 @@
 
     early = theirs(range(len(bunches) - 2))
     bounds = include(None, [level[c] for c in range(conds)] + early)
-    for i in ORDER:
-
-        @pl.when(sends[i])
-        def _():
-            for q in targets(i):
-                halo(i, q).wait_send()
-
     @pl.when(me == near)
     def _():
+        departed()
         for q in range(near):
             forward(q).wait_send()
 

time: 13.8 us -> 13.7 us (level)
  no operation moved by 1% of the time
where the time goes in v7:
time: 13.7 us; the launch traced here: 13.6 us
  Pallas kernels  12.9 us (94%)
  between operations  0.64 us (5%)
    pallas_call x1, Pallas kernels, on_device(): pl.pallas_call(scoped, out_shape=(out, out), in_specs=[anywhere] * 7, out...  12.2 us
    pallas_call x1, Pallas kernels, on_device(): pl.pallas_call(finish, out_shape=(out, out), in_specs=[vmem] * 2, out_spe...  0.7 us

profile of v7, /device:TPU:0, one launch (start us, length us, event | category | flops | bytes accessed | tf_op | source)
XLA Modules:
  0.0 13.6 jit_solution(10550159957504944303)
XLA Ops:
  0.6 12.2 %shard_map.86 = (f32[1,128,256]{2,1,0:T(8,128)S(1)}, f32[1,128,256]{2,1,0:T(8,128)S(1)}) custom-call(bf16[1,256,256]{2,1,0:T(8,128)(2,1)} %refs_0_.1, bf16[4,24,64,128]{3,2,1,0:T(8,128)(2,1)} %refs_1_.1, f32[4,24]{1,0:T(4,128)} %refs_2_.1, f32[4]{0:T(128)} %refs_3_.1, f32[4]{0:T(128)} %refs_4_.1, bf16[384,256]{1,0:T(8,128)(2,1)} %constant.4.clone.refs_5_, ...), custom_call_target="tpu_custom_call" | custom-call | tf_op jit(solution)/shard_map/pallas_call | solution.py:495
  12.9 0.7 %shard_map.87 = (f32[1,128,256]{2,1,0:T(8,128)}, f32[1,128,256]{2,1,0:T(8,128)}) custom-call(f32[1,128,256]{2,1,0:T(8,128)S(1)} %get-tuple-element.4.high, f32[1,128,256]{2,1,0:T(8,128)S(1)} %get-tuple-element.5.low), custom_call_target="tpu_custom_call" | custom-call | tf_op jit(solution)/shard_map/pallas_call | solution.py:525

commit v8 on v7

--- a/solution.py
+++ b/solution.py
@@ -418,7 +418,11 @@
                 continue
             part = jnp.concatenate([wide[:, j * grid : (j + 1) * grid] for j in some], axis=0)
             high, low = high_low(part)
-            blurred = dot(jnp.concatenate([high, high, low], axis=1), col_part)
+            part = jnp.concatenate([high, high, low], axis=1)
+            cut = len(part) if len(values) > 1 else len(part) // 2
+            blurred = jnp.concatenate(
+                [dot(part[n : n + cut], col_part) for n in range(0, len(part), cut)], axis=0
+            )
             for j in range(len(some)):
                 one = blurred[j * share : (j + 1) * share]
                 bounds = (one, one) if bounds is None else (
@@ -437,15 +441,26 @@
 
     early = theirs(range(len(bunches) - 2))
     bounds = include(None, [level[c] for c in range(conds)] + early)
+    late_bunches = list(range(max(len(bunches) - 2, 0), len(bunches)))
+
+    def conclude(rounds):
+        result = bounds
+        for numbers in rounds:
+            result = include(result, theirs(numbers))
+        high_out[0] = result[0]
+        low_out[0] = result[1]
+
     @pl.when(me == near)
     def _():
         departed()
         for q in range(near):
             forward(q).wait_send()
-
-    bounds = include(bounds, theirs(range(max(len(bunches) - 2, 0), len(bunches))))
-    high_out[0] = bounds[0]
-    low_out[0] = bounds[1]
+        conclude([[number] for number in late_bunches])
+
+    @pl.when(me != near)
+    def _():
+        conclude([late_bunches])
+
     for step in range(1, n_cond):
         for number in range(len(bunches)):
             swap(number, step).wait_send()

time: 13.7 us -> 13.7 us (level)
  no operation moved by 1% of the time
where the time goes in v8:
time: 13.7 us; the launch traced here: 13.5 us
  Pallas kernels  12.9 us (94%)
  between operations  0.64 us (5%)
    pallas_call x1, Pallas kernels, on_device(): pl.pallas_call(scoped, out_shape=(out, out), in_specs=[anywhere] * 7, out...  12.2 us
    pallas_call x1, Pallas kernels, on_device(): pl.pallas_call(finish, out_shape=(out, out), in_specs=[vmem] * 2, out_spe...  0.7 us

profile of v8, /device:TPU:0, one launch (start us, length us, event | category | flops | bytes accessed | tf_op | source)
XLA Modules:
  0.0 13.5 jit_solution(10773881130578928407)
XLA Ops:
  0.6 12.2 %shard_map.86 = (f32[1,128,256]{2,1,0:T(8,128)S(1)}, f32[1,128,256]{2,1,0:T(8,128)S(1)}) custom-call(bf16[1,256,256]{2,1,0:T(8,128)(2,1)} %refs_0_.1, bf16[4,24,64,128]{3,2,1,0:T(8,128)(2,1)} %refs_1_.1, f32[4,24]{1,0:T(4,128)} %refs_2_.1, f32[4]{0:T(128)} %refs_3_.1, f32[4]{0:T(128)} %refs_4_.1, bf16[384,256]{1,0:T(8,128)(2,1)} %constant.4.clone.refs_5_, ...), custom_call_target="tpu_custom_call" | custom-call | tf_op jit(solution)/shard_map/pallas_call | solution.py:510
  12.8 0.7 %shard_map.87 = (f32[1,128,256]{2,1,0:T(8,128)}, f32[1,128,256]{2,1,0:T(8,128)}) custom-call(f32[1,128,256]{2,1,0:T(8,128)S(1)} %get-tuple-element.4.high, f32[1,128,256]{2,1,0:T(8,128)S(1)} %get-tuple-element.5.low), custom_call_target="tpu_custom_call" | custom-call | tf_op jit(solution)/shard_map/pallas_call | solution.py:540
